TPU v7x, 32 devices: a whole 2x2x4 slice. The times are simulated.
32 devices in a mesh: gx: 4 (over y, x), gy: 4 (over z), gz: 2 (over core).
Axes of the slice: x: 2, y: 2, z: 4, core: 2. Of those that a mesh axis runs over, the one named last changes fastest.
Arguments:
- grads: float32 [4, 4, 2, 160, 4096], P('gx', 'gy', 'gz'), may hold values from -6 to 6
- peer_table: int32 [4], replicated, may hold values from 0 to 3, each once
- layer_offsets: int32 [2], replicated, may hold values from 0 to 96, as said below
Outputs:
- averaged: float32 [4, 4, 2, 128, 4096], P('gx', 'gy', 'gz')
Inputs may be any that keep to these rules, and one draw needn't show every extreme that they name: layer_offsets[l] is a multiple of 8 between l * (80) and l * 80 + 16; the last layer's offset is the largest of these.
All inputs are finite; a program needn't handle non-finite values.
Results may differ from a plain program's by a relative error of at most 0.00002.
Values sent between devices are 32-bit elements; how exact they have to be, the bound alone decides.
A program may use at most 64 MiB of HBM per device.

v0:
```python
import jax
import jax.numpy as jnp
from jax import lax
from jax.sharding import PartitionSpec as P

ROWS = 64
LAYERS = 2


def on_device(grads, peer_table, layer_offsets):
    buffer = grads[0, 0, 0]
    pieces = [lax.dynamic_slice_in_dim(buffer, layer_offsets[i], ROWS, 0) for i in range(LAYERS)]
    packed = jnp.concatenate(pieces, axis=0)
    count_y = lax.axis_size("gy")
    group_b = min(8, count_y)
    group_a = lax.axis_size("gx") * (count_y // group_b)
    places = jnp.arange(count_y, dtype=jnp.int32)
    onehot = (peer_table[:, None] == places[None, :]).astype(jnp.int32)
    inverse = jnp.sum(onehot * places[:, None], axis=0)
    spread = lax.all_to_all(packed[None], "gy", split_axis=1, concat_axis=0, tiled=True)
    current = jnp.take(spread, peer_table, axis=0)
    total_c = lax.psum(current, "gz")
    current = 0.5 * current + 0.5 / lax.axis_size("gz") * total_c
    block_rows = current.shape[1]
    width = current.shape[2]
    split = current.reshape(count_y // group_b, group_b, block_rows, width)
    total_b = jnp.sum(split, axis=1, keepdims=True)
    split = 0.5 * split + 0.5 / group_b * total_b
    local_a = jnp.sum(split, axis=0, keepdims=True)
    total_a = lax.psum(local_a, "gx")
    split = 0.5 * split + 0.5 / group_a * total_a
    current = jnp.take(split.reshape(count_y, block_rows, width), inverse, axis=0)
    result = lax.all_to_all(current, "gy", split_axis=0, concat_axis=1, tiled=True)[0]
    return result[None, None, None]


def solution(mesh):
    placed = (P("gx", "gy", "gz", None, None), P(), P())
    return jax.shard_map(
        on_device,
        mesh=mesh,
        in_specs=placed,
        out_specs=P("gx", "gy", "gz", None, None),
        check_vma=False,
    )
```

profile of v0, /device:TPU:0, one launch (start us, length us, event | category | flops | bytes accessed | tf_op | source)
XLA Modules:
  0.0 241.6 jit_solution(17327902413841182848)
XLA Ops:
  6.5 1.3 fusion.3
  11.5 1.8 dynamic-slice_bitcast_fusion.1
  13.3 0.1 pad_maximum_fusion
  13.5 3.7 %broadcast_in_dim.11 = f32[1,128,4096]{2,0,1:T(1,128)} reshape(f32[128,4096]{1,0:T(8,128)S(1)} %pad_maximum_fusion) | data formatting | bytes 4194304 | tf_op jit(solution)/shard_map/broadcast_in_dim | solution.py:20
  17.2 0.0 copy-start.1
  17.2 6.5 %all-to-all-start = ((f32[1,128,4096]{2,0,1:T(1,128)}), f32[1,128,4096]{2,0,1:T(1,128)S(1)}, u32[]{:S(2)}, u32[]{:S(2)}) async-start(f32[1,128,4096]{2,0,1:T(1,128)} %broadcast_in_dim.11), calls=%async_computation | async-start | bytes 4194304 | tf_op jit(solution)/shard_map/all_to_all | solution.py:20
  23.6 0.0 all-reduce.3.cloned.1.call-start
  23.6 0.0 copy-done.1
  23.7 48.2 %all-to-all-done = f32[1,128,4096]{2,0,1:T(1,128)S(1)} async-done(((f32[1,128,4096]{2,0,1:T(1,128)}), f32[1,128,4096]{2,0,1:T(1,128)S(1)}, u32[]{:S(2)}, u32[]{:S(2)}) %all-to-all-start) | async-done | bytes 2097184 | tf_op jit(solution)/shard_map/all_to_all | solution.py:20
  71.8 3.0 %copy.4 = f32[1,128,4096]{2,1,0:T(8,128)} copy(f32[1,128,4096]{2,0,1:T(1,128)S(1)} %all-to-all-done) | data formatting | bytes 4194304
  74.8 2.3 gather_fusion
  77.1 1.6 broadcast_select_fusion.1
  78.7 0.0 all-reduce.3.cloned.1.call-update
  78.7 0.0 all-reduce.5.cloned.1.call-start
  78.7 20.5 %all-reduce.3.cloned.1.call-done = f32[4,32,4096]{2,1,0:T(8,128)} async-done(((f32[4,32,4096]{2,1,0:T(8,128)}), f32[4,32,4096]{2,1,0:T(8,128)}) %all-reduce.3.cloned.1.call-update) | async-done | bytes 2097168 | tf_op jit(solution)/shard_map/psum | solution.py:22
  99.2 0.0 copy-start
  99.2 2.3 fusion.2
  101.6 0.0 copy-done
  101.6 1.8 fusion.1
  103.4 0.0 all-reduce.5.cloned.1.call-update
  103.4 0.1 select_reduce_fusion
  103.5 70.7 %all-reduce.5.cloned.1.call-done = f32[1,4,32,4096]{3,2,1,0:T(8,128)} async-done(((f32[1,4,32,4096]{3,2,1,0:T(8,128)}), f32[1,4,32,4096]{3,2,1,0:T(8,128)}) %all-reduce.5.cloned.1.call-update) | async-done | bytes 2097168 | tf_op jit(solution)/shard_map/psum | solution.py:30
  174.3 4.2 %fusion = f32[4,32,4096]{2,1,0:T(8,128)} fusion(f32[1,4,32,4096]{3,2,1,0:T(8,128)} %all-reduce.5.cloned.1.call-done, f32[32,4096]{1,0:T(8,128)S(1)} %broadcast_multiply_fusion, f32[4,32,4096]{2,1,0:T(8,128)} %all-reduce.3.cloned.1.call-done, f32[4,32,4096]{2,1,0:T(8,128)S(1)} %gather_fusion, pred[4]{0:T(512)(128)(4,1)S(1)} %compare_and_fusion.1), kind=kLoop, calls=%fused_computation.4 | loop fusion | flops 4718592 | bytes 8912900 | tf_op jit(solution)/shard_map/reshape | solution.py:32
  178.5 2.3 gather_fusion.1
  180.8 0.3 broadcast_select_fusion
  181.0 52.4 %all_to_all.21 = f32[4,32,4096]{2,1,0:T(8,128)S(1)} all-to-all(f32[4,32,4096]{2,1,0:T(8,128)S(1)} %broadcast_select_fusion), channel_id=1, replica_groups=mesh['gx'=4,'gy'=4,'gz'=2] {'gy'}, dimensions={0} | all-to-all | bytes 4194304 | tf_op jit(solution)/shard_map/all_to_all | solution.py:33
  233.5 1.3 copy.8
  (7 shorter events, 0.1 us)
Async XLA Ops:
  17.2 6.5 %copy-start.1 = (s32[4]{0:T(128)S(1)}, s32[4]{0:T(128)}, u32[]{:S(2)}) copy-start(s32[4]{0:T(128)} %param.6) | copy-start | bytes 52
  17.2 54.7 %all-to-all-start = ((f32[1,128,4096]{2,0,1:T(1,128)}), f32[1,128,4096]{2,0,1:T(1,128)S(1)}, u32[]{:S(2)}, u32[]{:S(2)}) async-start(f32[1,128,4096]{2,0,1:T(1,128)} %broadcast_in_dim.11), calls=%async_computation | async-start | bytes 4194304 | tf_op jit(solution)/shard_map/all_to_all | solution.py:20
  23.6 75.6 %all-reduce.3.cloned.1.call-start = ((), (), s32[]{:S(2)}) async-start(), calls=%async_computation.2 | async-start | bytes 4194304 | tf_op jit(solution)/shard_map/psum | solution.py:22
  78.7 95.6 %all-reduce.5.cloned.1.call-start = ((), (), s32[]{:S(2)}) async-start(), calls=%async_computation.3 | async-start | bytes 4194304 | tf_op jit(solution)/shard_map/psum | solution.py:30
  99.2 2.3 copy-start
Sparse Core Ops, SparseCore 0:
  78.8 20.3 all-reduce.2
  103.6 70.6 all-reduce.4
where the time goes:
time: 242 us
  waiting for transfers between devices  139 us (57%)
  blocking collectives  52.4 us (22%)
  between operations  17.1 us (7%)
  local copies, waits for them, and re-layouts  15.7 us (6%)
  other arithmetic  10.5 us (4%)
  starting transfers between devices  6.52 us (3%)
    psum x1, waiting for transfers between devices, on_device(): total_a = lax.psum(local_a, 'gx')  70.7 us
    all_to_all x1, blocking collectives, on_device(): lax.all_to_all(current, 'gy', split_axis=0, concat_axis=1, tiled=True)[0]  52.4 us
    all_to_all x1, waiting for transfers between devices, on_device(): lax.all_to_all(packed[None], 'gy', split_axis=1, concat_axis=0, tiled=True)  48.2 us
    psum x1, waiting for transfers between devices, on_device(): total_c = lax.psum(current, 'gz')  20.5 us
    all_to_all x1, starting transfers between devices, on_device(): lax.all_to_all(packed[None], 'gy', split_axis=1, concat_axis=0, tiled=True)  6.48 us
  transfers between devices with their start and end apart: 3, of which 3 were waited for; matrix products, arithmetic and copies ran while one was open for 0% of the time, Pallas kernels for 0%

commit v1 on v0

--- a/solution.py
+++ b/solution.py
@@ -17,7 +17,19 @@
     places = jnp.arange(count_y, dtype=jnp.int32)
     onehot = (peer_table[:, None] == places[None, :]).astype(jnp.int32)
     inverse = jnp.sum(onehot * places[:, None], axis=0)
-    spread = lax.all_to_all(packed[None], "gy", split_axis=1, concat_axis=0, tiled=True)
+    ways, here = (lax.axis_size("gy"), lax.axis_index("gy"))
+    width_2 = packed[None].shape[1] // ways
+    shape = list(packed[None].shape)
+    shape[1] = width_2
+    height = shape[0]
+    shape[0] = height * ways
+    full = jnp.zeros(shape, packed[None].dtype)
+    for mask in range(ways):
+        part = lax.dynamic_slice_in_dim(packed[None], (here ^ mask) * width_2, width_2, axis=1)
+        if mask:
+            part = lax.ppermute(part, "gy", [(d, d ^ mask) for d in range(ways)])
+        full = lax.dynamic_update_slice_in_dim(full, part, (here ^ mask) * height, axis=0)
+    spread = full
     current = jnp.take(spread, peer_table, axis=0)
     total_c = lax.psum(current, "gz")
     current = 0.5 * current + 0.5 / lax.axis_size("gz") * total_c

time: 242 us -> 234 us (0.967)
  waiting for transfers between devices: 139 us -> 132 us
    all_to_all x1 -> x0, waiting for transfers between devices: 48.2 us -> none  [on_device(): lax.all_to_all(packed[None], 'gy', split_axis=1, concat_axis=0, tiled=True)]
    ppermute x0 -> x3, waiting for transfers between devices: none -> 31.5 us  [on_device(): part = lax.ppermute(part, 'gy', [(d, d ^ mask) for d in range(ways)])]
    psum x1, waiting for transfers between devices: 20.5 us -> 29.7 us  [on_device(): total_c = lax.psum(current, 'gz')]
    all_to_all x1 -> x0, starting transfers between devices: 6.48 us -> none  [on_device(): lax.all_to_all(packed[None], 'gy', split_axis=1, concat_axis=0, tiled=True)]
    ppermute x0 -> x3, starting transfers between devices: none -> 5.64 us  [on_device(): part = lax.ppermute(part, 'gy', [(d, d ^ mask) for d in range(ways)])]
    dynamic_update_slice x0 -> x3, local copies, waits for them, and re-layouts: none -> 3.53 us  [on_device(): lax.dynamic_update_slice_in_dim(full, part, (here ^ mask) * height, axis=0)]
    unnamed x6 -> x5, local copies, waits for them, and re-layouts: 4.28 us -> 1.33 us
  transfers between devices with their start and end apart: 3 -> 5, of which waited for: 3 -> 4; matrix products, arithmetic and copies ran while one was open for 0% -> 2% of each run, Pallas kernels for 0% -> 0%
where the time goes in v1:
time: 234 us
  waiting for transfers between devices  132 us (56%)
  blocking collectives  52.4 us (22%)
  between operations  17.4 us (7%)
  local copies, waits for them, and re-layouts  14.1 us (6%)
  other arithmetic  12.5 us (5%)
  starting transfers between devices  5.69 us (2%)
    psum x1, waiting for transfers between devices, on_device(): total_a = lax.psum(local_a, 'gx')  70.7 us
    all_to_all x1, blocking collectives, on_device(): lax.all_to_all(current, 'gy', split_axis=0, concat_axis=1, tiled=True)[0]  52.4 us
    ppermute x3, waiting for transfers between devices, on_device(): part = lax.ppermute(part, 'gy', [(d, d ^ mask) for d in range(ways)])  31.5 us
    psum x1, waiting for transfers between devices, on_device(): total_c = lax.psum(current, 'gz')  29.7 us
    ppermute x3, starting transfers between devices, on_device(): part = lax.ppermute(part, 'gy', [(d, d ^ mask) for d in range(ways)])  5.64 us
  transfers between devices with their start and end apart: 5, of which 4 were waited for; matrix products, arithmetic and copies ran while one was open for 2% of the time, Pallas kernels for 0%

profile of v1, /device:TPU:0, one launch (start us, length us, event | category | flops | bytes accessed | tf_op | source)
XLA Modules:
  0.0 233.9 jit_solution(16110481943765736754)
XLA Ops:
  6.5 0.0 all-reduce.3.cloned.1.call-start
  6.5 1.3 fusion.12
  11.7 1.8 dynamic-slice_bitcast_fusion
  13.6 0.0 copy-start.1
  13.6 1.3 fusion.3
  14.8 3.1 %collective-permute-start = (f32[1,32,4096]{2,1,0:T(8,128)}, f32[1,32,4096]{2,1,0:T(8,128)}, u32[]{:S(2)}, u32[]{:S(2)}) collective-permute-start(f32[1,32,4096]{2,1,0:T(8,128)} %get-tuple-element.9), channel_id=1, source_target_pairs={{0,2},{2,0},{4,6},{6,4},{1,3},{3,1},{5,7},{7,5},{8,10},{10,8},{12,... | collective-permute-start | bytes 1572872 | tf_op jit(solution)/shard_map/ppermute | solution.py:30
  17.9 2.6 %collective-permute-start.1 = (f32[1,32,4096]{2,1,0:T(8,128)}, f32[1,32,4096]{2,1,0:T(8,128)S(1)}, u32[]{:S(2)}, u32[]{:S(2)}) collective-permute-start(f32[1,32,4096]{2,1,0:T(8,128)} %get-tuple-element.10), channel_id=1, source_target_pairs={{0,4},{2,6},{4,0},{6,2},{1,5},{3,7},{5,1},{7,3},{8,12},{10,14},{12... | collective-permute-start | bytes 1572872 | tf_op jit(solution)/shard_map/ppermute | solution.py:30
  20.5 0.0 collective-permute-start.2
  20.5 0.0 copy-done.1
  20.5 1.5 broadcast_in_dim.8
  22.1 0.9 fusion.6
  22.9 17.7 %collective-permute-done = f32[1,32,4096]{2,1,0:T(8,128)} collective-permute-done((f32[1,32,4096]{2,1,0:T(8,128)}, f32[1,32,4096]{2,1,0:T(8,128)}, u32[]{:S(2)}, u32[]{:S(2)}) %collective-permute-start) | collective-permute-done | bytes 524320 | tf_op jit(solution)/shard_map/ppermute | solution.py:30
  40.6 1.9 constant_dynamic-update-slice_fusion.2
  42.5 13.8 %collective-permute-done.1 = f32[1,32,4096]{2,1,0:T(8,128)S(1)} collective-permute-done((f32[1,32,4096]{2,1,0:T(8,128)}, f32[1,32,4096]{2,1,0:T(8,128)S(1)}, u32[]{:S(2)}, u32[]{:S(2)}) %collective-permute-start.1) | collective-permute-done | bytes 524320 | tf_op jit(solution)/shard_map/ppermute | solution.py:30
  56.3 0.8 constant_dynamic-update-slice_fusion.1
  57.1 0.0 collective-permute-done.2
  57.1 0.8 constant_dynamic-update-slice_fusion
  57.9 2.3 gather_fusion
  60.2 1.6 broadcast_select_fusion.1
  61.8 0.0 all-reduce.3.cloned.1.call-update
  61.8 0.0 all-reduce.5.cloned.1.call-start
  61.9 29.7 %all-reduce.3.cloned.1.call-done = f32[4,32,4096]{2,1,0:T(8,128)} async-done(((f32[4,32,4096]{2,1,0:T(8,128)}), f32[4,32,4096]{2,1,0:T(8,128)}) %all-reduce.3.cloned.1.call-update) | async-done | bytes 2097168 | tf_op jit(solution)/shard_map/psum | solution.py:34
  91.5 0.0 copy-start
  91.5 2.3 fusion.11
  93.9 0.0 copy-done
  93.9 1.8 fusion.1
  95.7 0.0 all-reduce.5.cloned.1.call-update
  95.7 0.1 select_reduce_fusion
  95.9 70.7 %all-reduce.5.cloned.1.call-done = f32[1,4,32,4096]{3,2,1,0:T(8,128)} async-done(((f32[1,4,32,4096]{3,2,1,0:T(8,128)}), f32[1,4,32,4096]{3,2,1,0:T(8,128)}) %all-reduce.5.cloned.1.call-update) | async-done | bytes 2097168 | tf_op jit(solution)/shard_map/psum | solution.py:42
  166.6 4.2 %fusion = f32[4,32,4096]{2,1,0:T(8,128)} fusion(f32[1,4,32,4096]{3,2,1,0:T(8,128)} %all-reduce.5.cloned.1.call-done, f32[32,4096]{1,0:T(8,128)S(1)} %broadcast_multiply_fusion, f32[4,32,4096]{2,1,0:T(8,128)} %all-reduce.3.cloned.1.call-done, f32[4,32,4096]{2,1,0:T(8,128)S(1)} %gather_fusion, pred[4]{0:T(512)(128)(4,1)S(1)} %compare_and_fusion.1), kind=kLoop, calls=%fused_computation.11 | loop fusion | flops 4718592 | bytes 8912900 | tf_op jit(solution)/shard_map/reshape | solution.py:44
  170.8 2.3 gather_fusion.1
  173.1 0.3 broadcast_select_fusion
  173.3 52.4 %all_to_all.4 = f32[4,32,4096]{2,1,0:T(8,128)S(1)} all-to-all(f32[4,32,4096]{2,1,0:T(8,128)S(1)} %broadcast_select_fusion), channel_id=1, replica_groups=mesh['gx'=4,'gy'=4,'gz'=2] {'gy'}, dimensions={0} | all-to-all | bytes 4194304 | tf_op jit(solution)/shard_map/all_to_all | solution.py:45
  225.8 1.3 copy.11
  (7 shorter events, 0.1 us)
Async XLA Ops:
  6.5 85.0 %all-reduce.3.cloned.1.call-start = ((), (), s32[]{:S(2)}) async-start(), calls=%async_computation.1 | async-start | bytes 4194304 | tf_op jit(solution)/shard_map/psum | solution.py:34
  13.6 6.9 %copy-start.1 = (s32[4]{0:T(128)S(1)}, s32[4]{0:T(128)}, u32[]{:S(2)}) copy-start(s32[4]{0:T(128)} %param.6) | copy-start | bytes 52
  14.8 25.8 %collective-permute-start = (f32[1,32,4096]{2,1,0:T(8,128)}, f32[1,32,4096]{2,1,0:T(8,128)}, u32[]{:S(2)}, u32[]{:S(2)}) collective-permute-start(f32[1,32,4096]{2,1,0:T(8,128)} %get-tuple-element.9), channel_id=1, source_target_pairs={{0,2},{2,0},{4,6},{6,4},{1,3},{3,1},{5,7},{7,5},{8,10},{10,8},{12,... | collective-permute-start | bytes 1572872 | tf_op jit(solution)/shard_map/ppermute | solution.py:30
  17.9 38.4 %collective-permute-start.1 = (f32[1,32,4096]{2,1,0:T(8,128)}, f32[1,32,4096]{2,1,0:T(8,128)S(1)}, u32[]{:S(2)}, u32[]{:S(2)}) collective-permute-start(f32[1,32,4096]{2,1,0:T(8,128)} %get-tuple-element.10), channel_id=1, source_target_pairs={{0,4},{2,6},{4,0},{6,2},{1,5},{3,7},{5,1},{7,3},{8,12},{10,14},{12... | collective-permute-start | bytes 1572872 | tf_op jit(solution)/shard_map/ppermute | solution.py:30
  20.5 36.6 %collective-permute-start.2 = (f32[1,32,4096]{2,1,0:T(8,128)}, f32[1,32,4096]{2,1,0:T(8,128)S(1)}, u32[]{:S(2)}, u32[]{:S(2)}) collective-permute-start(f32[1,32,4096]{2,1,0:T(8,128)} %get-tuple-element.8), channel_id=1, source_target_pairs={{0,6},{2,4},{4,2},{6,0},{1,7},{3,5},{5,3},{7,1},{8,14},{10,12},{12... | collective-permute-start | bytes 1572872 | tf_op jit(solution)/shard_map/ppermute | solution.py:30
  61.8 104.7 %all-reduce.5.cloned.1.call-start = ((), (), s32[]{:S(2)}) async-start(), calls=%async_computation.2 | async-start | bytes 4194304 | tf_op jit(solution)/shard_map/psum | solution.py:42
  91.5 2.3 copy-start
Sparse Core Ops, SparseCore 0:
  61.9 29.5 all-reduce.2
  95.9 70.6 all-reduce.4
